TPU v7x, 32 devices: a whole 2x2x4 slice. The times are simulated.
32 devices in a mesh: rep: 2 (over x), stretch: 2 (over core), tp: 8 (over z, y).
Axes of the slice: x: 2, y: 2, z: 4, core: 2. Of those that a mesh axis runs over, the one named last changes fastest.
Arguments:
- query: bfloat16 [4, 512, 3072], P(('rep', 'stretch'), 'tp'), parts along dimension 0, may hold values from -64 to 64
- stretch_kv: bfloat16 [2, 4, 512, 3072], P(None, ('rep', 'stretch'), 'tp'), parts along dimension 1, may hold values from -6 to 6
- history_kv: bfloat16 [2, 4096, 3072], P(None, ('rep', 'tp')), parts along dimension 1, may hold values from -6 to 6
- block_mask: int32 [4, 4, 8], P(('rep', 'stretch')), parts along dimension 0, may hold values from 0 to 1, as said below
- noise_level: int32 [4], P(('rep', 'stretch')), parts along dimension 0, may hold values from 0 to 999
- history_blocks: int32 [2], P('rep'), parts along dimension 0, may hold values from 1 to 16
- out_weight: bfloat16 [3072, 6144], P(None, 'tp'), may hold values from -0.109375 to 0.109375
- gate_table: float32 [1000, 6144], P(None, 'tp'), may hold values from -6 to 6
Outputs:
- mixed: bfloat16 [4, 512, 6144], P(('rep', 'stretch'), None, 'tp'), parts along dimension 0
There are 2 independent parts, one for each index of `rep`. A program takes and returns all parts, laid end to end along the dimension named above; an argument that names none is the same for every part. Nothing has to cross between parts.
Inputs may be any that keep to these rules, and one draw needn't show every extreme that they name: block_mask[c, i, 4 + i] = 1 for every query block i; block_mask[0, i, j] = 0 for j < 4.
All inputs are finite; a program needn't handle non-finite values.
Results may differ from a plain program's by a relative error of at most 0.0049.
Values may be sent and summed in bfloat16 or wider, within the bound.
A program may use at most 128 MiB of HBM per device.

v0:
```python
import math

import jax
import jax.numpy as jnp
from jax import lax
from jax.sharding import PartitionSpec as P

H = 24
HD = 128
BLK = 128


NEGATIVE = -1e30


def shifted(value, axis, steps):
    count = lax.axis_size(axis)
    first, last = (max(0, -steps), min(count, count - steps))
    return lax.ppermute(value, axis, [(source, source + steps) for source in range(first, last)])


def head_block(queries, key_rows, value_rows, allowed):
    key_count = key_rows.shape[0]
    head_count = queries.shape[1]
    key_heads = key_rows.reshape(key_count, head_count, HD)
    scores = jnp.einsum("qhd,khd->qhk", queries, key_heads, preferred_element_type=jnp.float32) * (
        1.0 / math.sqrt(HD)
    )
    scores = jnp.where(allowed[:, None, :], scores, NEGATIVE)
    row_peak = jnp.max(scores, axis=2)
    weights = jnp.where(allowed[:, None, :], jnp.exp(scores - row_peak[:, :, None]), 0.0)
    weight_sum = jnp.sum(weights, axis=2)
    output = None
    value_heads = value_rows.reshape(key_count, head_count, HD).astype(jnp.float32)
    output = jnp.einsum("qhk,khd->qhd", weights, value_heads, precision=lax.Precision.HIGHEST)
    return (row_peak, weight_sum, output)


def combine(earlier, later):
    row_peak = jnp.maximum(earlier[0], later[0])
    scale_one = jnp.exp(earlier[0] - row_peak)
    scale_two = jnp.exp(later[0] - row_peak)
    weight_sum = earlier[1] * scale_one + later[1] * scale_two
    output = None
    output = earlier[2] * scale_one[:, :, None] + later[2] * scale_two[:, :, None]
    return (row_peak, weight_sum, output)


def column_table(columns, block_count):
    return (columns[:, None] == jnp.arange(2 * block_count, dtype=jnp.int32)[None, :]).astype(
        jnp.float32
    )


def attend_all(
    queries,
    query_positions,
    fresh_keys,
    fresh_values,
    fresh_hot,
    mask_table,
    history_pair,
    history_live,
    span,
):
    row_count = queries.shape[0]
    head_count = queries.shape[1]
    block_count = mask_table.shape[0]
    query_hot = (
        (query_positions // BLK)[:, None] == jnp.arange(block_count, dtype=jnp.int32)[None, :]
    ).astype(jnp.float32)
    fresh_allowed = jnp.dot(jnp.dot(query_hot, mask_table), fresh_hot.T) > 0.5
    base_peak = jnp.full((row_count, head_count), NEGATIVE, jnp.float32)
    skipped = (
        base_peak,
        jnp.zeros((row_count, head_count), jnp.float32),
        jnp.zeros((row_count, head_count, HD), jnp.float32),
    )
    result = head_block(queries, fresh_keys, fresh_values, fresh_allowed)
    for sub_block in range(history_pair.shape[1] // span):
        lower_row = sub_block * span
        key_rows = history_pair[0, lower_row : lower_row + span]
        value_rows = history_pair[1, lower_row : lower_row + span]
        live_rows = history_live[lower_row : lower_row + span]
        allowed = jnp.broadcast_to(live_rows[None, :], (row_count, span))
        block_part = lax.cond(
            jnp.any(live_rows),
            lambda: head_block(queries, key_rows, value_rows, allowed),
            lambda: skipped,
        )
        result = combine(result, block_part)
    return result


def on_device(
    query, stretch_kv, history_kv, block_mask, noise_level, history_blocks, out_weight, gate_table
):
    tp_count = lax.axis_size("tp")
    tp_index = lax.axis_index("tp")
    local_rows = query.shape[1]
    feature_width = query.shape[2]
    history_rows = history_kv.shape[1]
    block_count = block_mask.shape[1]
    own_pair = stretch_kv[:, 0]
    older_pair = shifted(own_pair, "stretch", 1)
    mask_table = block_mask[0].astype(jnp.float32)
    live_limit = history_blocks[0] * BLK
    fresh_keys = jnp.concatenate([older_pair[0], own_pair[0]], 0)
    fresh_values = jnp.concatenate([older_pair[1], own_pair[1]], 0)
    own_positions = tp_index * local_rows + jnp.arange(local_rows, dtype=jnp.int32)
    fresh_hot = column_table(
        jnp.concatenate([own_positions // BLK, block_count + own_positions // BLK], 0), block_count
    )
    history_positions = tp_index * history_rows + jnp.arange(history_rows, dtype=jnp.int32)
    history_live = history_positions < live_limit
    piece = lax.all_gather(query[0], "tp", axis=0, tiled=True)
    row_count = piece.shape[0]
    positions = jnp.arange(row_count, dtype=jnp.int32)
    row_peak, weight_sum, output = attend_all(
        piece.reshape(row_count, H, HD),
        positions,
        fresh_keys,
        fresh_values,
        fresh_hot,
        mask_table,
        history_kv,
        history_live,
        BLK,
    )
    got_outputs, got_peaks, got_sums = (
        lax.all_to_all(
            output.reshape(tp_count, local_rows, H, HD),
            "tp",
            split_axis=0,
            concat_axis=0,
            tiled=True,
        ),
        lax.all_to_all(
            row_peak.reshape(tp_count, local_rows, H), "tp", split_axis=0, concat_axis=0, tiled=True
        ),
        lax.all_to_all(
            weight_sum.reshape(tp_count, local_rows, H),
            "tp",
            split_axis=0,
            concat_axis=0,
            tiled=True,
        ),
    )
    overall = jnp.max(got_peaks, axis=0)
    factor = jnp.exp(got_peaks - overall[None])
    merged_sum = jnp.sum(got_sums * factor, axis=0)
    merged = jnp.sum(got_outputs * factor[:, :, :, None], axis=0) / merged_sum[:, :, None]
    attended = merged.reshape(local_rows, feature_width).astype(jnp.bfloat16)
    projected = jnp.dot(
        lax.all_gather(attended, "tp", axis=0, tiled=True),
        out_weight,
        preferred_element_type=jnp.float32,
    )
    level_hot = (jnp.arange(gate_table.shape[0], dtype=jnp.int32) == noise_level[0]).astype(
        jnp.float32
    )[None, :]
    gate_row = jnp.dot(level_hot, gate_table, precision=lax.Precision.HIGHEST)
    return (projected * gate_row).astype(jnp.bfloat16)[None]


def solution(mesh):
    return jax.shard_map(
        on_device,
        mesh=mesh,
        in_specs=(
            P(("rep", "stretch"), "tp", None),
            P(None, ("rep", "stretch"), "tp", None),
            P(None, ("rep", "tp"), None),
            P(("rep", "stretch"), None, None),
            P(("rep", "stretch")),
            P("rep"),
            P(None, "tp"),
            P(None, "tp"),
        ),
        out_specs=P(("rep", "stretch"), None, "tp"),
        check_vma=False,
    )
```

profile of v0, /device:TPU:0, one launch (start us, length us, event | category | flops | bytes accessed | tf_op | source)
XLA Modules:
  0.0 404.0 jit_solution(16750470983532467193)
XLA Ops:
  6.5 0.7 all-gather.6.cloned.1.call-update
  7.3 3.4 collective-permute-start
  11.4 1.2 convolution_compare_fusion
  12.6 0.7 slice_reduce_fusion.1
  14.7 1.9 fusion.73
  16.8 1.9 fusion.72
  18.8 0.8 copy.90
  19.6 52.7 %all-gather.6.cloned.1.call-done = bf16[1,512,3072]{2,1,0:T(8,128)(2,1)} async-done(((bf16[1,64,3072]{2,1,0:T(8,128)(2,1)}), bf16[1,512,3072]{2,1,0:T(8,128)(2,1)}) %all-gather.6.cloned.1.call-update) | async-done | bytes 3145744 | tf_op jit(solution)/shard_map/all_gather | solution.py:116
  72.3 4.7 %copy.92 = bf16[1,512,3072]{1,2,0:T(8,128)(2,1)} copy(bf16[1,512,3072]{2,1,0:T(8,128)(2,1)} %all-gather.6.cloned.1.call-done) | data formatting | bytes 6291456 | tf_op jit(solution)/shard_map/all_gather | solution.py:116
  77.0 3.4 fusion.37
  80.4 2.7 fusion.38
  83.1 28.6 %conditional.3 = (f32[512,24]{0,1:T(8,128)}, f32[512,24]{0,1:T(8,128)}, f32[512,24,128]{0,2,1:T(8,128)}) conditional(s32[]{:T(128)} %convert_element_type.30, () %tuple.23, (pred[128]{0:T(512)(128)(4,1)S(1)}, bf16[2,256,3072]{2,1,0:T(8,128)(2,1)}, bf16[512,24,128]{0,2,1:T(8,128)(2,1)}) %tuple.60), branch_computations={%region_7.8_spmd, %region_8.11_spmd} | conditional | flops 2837422080 | bytes 52101528 | solution.py:86
  83.1 4.7 %copy.98 = bf16[2,256,3072]{1,2,0:T(8,128)(2,1)} copy(bf16[2,256,3072]{2,1,0:T(8,128)(2,1)} %get-tuple-element.59) | data formatting | bytes 6291456 | tf_op jit(solution)/shard_map
  87.8 1.5 fusion.71
  89.3 4.2 %bitcast_reduce_fusion.1 = (f32[512,24]{0,1:T(8,128)}, f32[24,128,512]{2,1,0:T(8,128)S(1)}) fusion(pred[128]{0:T(512)(128)(4,1)S(1)} %get-tuple-element.28, bf16[128,24,128]{0,2,1:T(8,128)(2,1)S(1)} %bitcast.110, bf16[512,24,128]{0,2,1:T(8,128)(2,1)} %get-tuple-element.60), kind=kOutput, calls=%fused_computation.18 | convolution fusion | flops 407359488 | bytes 10272896 | tf_op jit(solution)/shard_map/cond/branch_1_fun/qhd,khd->qhk/dot_general | solution.py:26
  93.5 3.1 fusion.21
  96.6 8.6 %fusion.28 = f32[512,24,128]{2,0,1:T(8,128)} fusion(bf16[128,24,128]{0,2,1:T(8,128)(2,1)S(1)} %bitcast.112, f32[24,128,512]{2,1,0:T(8,128)S(1)} %get-tuple-element.80, f32[512,24]{0,1:T(8,128)} %get-tuple-element.94, pred[128]{0:T(512)(128)(4,1)S(1)} %get-tuple-element.28), kind=kOutput, calls=%fused_computation.30 | convolution fusion | flops 2422210560 | bytes 13418624 | tf_op jit(solution)/shard_map/cond/branch_1_fun/qhk,khd->qhd/dot_general | solution.py:35
  105.1 6.6 %copy.119 = f32[512,24,128]{0,2,1:T(8,128)} copy(f32[512,24,128]{2,0,1:T(8,128)} %fusion.28) | data formatting | bytes 12582912 | tf_op jit(solution)/shard_map/cond | solution.py:86
  111.7 28.7 %conditional.2 = (f32[512,24]{0,1:T(8,128)}, f32[512,24]{0,1:T(8,128)}, f32[512,24,128]{0,2,1:T(8,128)}) conditional(s32[]{:T(128)} %convert_element_type.29, () %tuple.21, (pred[128]{0:T(512)(128)(4,1)S(1)}, bf16[2,256,3072]{2,1,0:T(8,128)(2,1)}, bf16[512,24,128]{0,2,1:T(8,128)(2,1)}) %tuple.61), branch_computations={%region_2.3_spmd, %region_3.6_spmd} | conditional | flops 2837422080 | bytes 52101528 | solution.py:86
  111.7 4.8 %copy.95 = bf16[2,256,3072]{1,2,0:T(8,128)(2,1)} copy(bf16[2,256,3072]{2,1,0:T(8,128)(2,1)} %get-tuple-element.56) | data formatting | bytes 6291456 | tf_op jit(solution)/shard_map
  116.5 1.5 fusion.70
  118.0 4.2 %bitcast_reduce_fusion = (f32[512,24]{0,1:T(8,128)}, f32[24,128,512]{2,1,0:T(8,128)S(1)}) fusion(pred[128]{0:T(512)(128)(4,1)S(1)} %get-tuple-element.25, bf16[128,24,128]{0,2,1:T(8,128)(2,1)S(1)} %bitcast.111, bf16[512,24,128]{0,2,1:T(8,128)(2,1)} %get-tuple-element.57), kind=kOutput, calls=%fused_computation.1 | convolution fusion | flops 407359488 | bytes 10272896 | tf_op jit(solution)/shard_map/cond/branch_1_fun/qhd,khd->qhk/dot_general | solution.py:26
  122.1 3.1 fusion.4
  125.2 8.6 %fusion.11 = f32[512,24,128]{2,0,1:T(8,128)} fusion(bf16[128,24,128]{0,2,1:T(8,128)(2,1)S(1)} %bitcast.113, f32[24,128,512]{2,1,0:T(8,128)S(1)} %get-tuple-element.76, f32[512,24]{0,1:T(8,128)} %get-tuple-element.100, pred[128]{0:T(512)(128)(4,1)S(1)} %get-tuple-element.25), kind=kOutput, calls=%fused_computation.13 | convolution fusion | flops 2422210560 | bytes 13418624 | tf_op jit(solution)/shard_map/cond/branch_1_fun/qhk,khd->qhd/dot_general | solution.py:35
  133.8 6.6 %copy.117 = f32[512,24,128]{0,2,1:T(8,128)} copy(f32[512,24,128]{2,0,1:T(8,128)} %fusion.11) | data formatting | bytes 12582912 | tf_op jit(solution)/shard_map/cond | solution.py:86
  140.4 1.7 multiply_add_fusion
  142.0 1.5 reshape.73
  143.6 1.5 copy.128
  145.1 1.6 reshape.80
  146.7 4.0 all-to-all-start.1
  150.7 1.2 copy.88
  151.9 2.2 copy.87
  154.1 0.9 reshape.74
  155.0 0.7 reshape.82
  155.7 1.8 all-to-all-done.1
  157.5 4.1 %all-to-all-start.2 = ((f32[8,1,1536]{2,1,0:T(1,128)}), f32[8,1,1536]{2,1,0:T(1,128)S(1)}, u32[]{:S(2)}, u32[]{:S(2)}) async-start(f32[8,1,1536]{2,1,0:T(1,128)} %reshape.82), calls=%async_computation.2 | async-start | bytes 98304 | tf_op jit(solution)/shard_map/all_to_all | solution.py:141
  161.6 15.7 %fusion.36 = f32[512,24,128]{0,2,1:T(8,128)} fusion(f32[512,24,128]{0,2,1:T(8,128)} %get-tuple-element.62, f32[512,24,128]{0,2,1:T(8,128)} %get-tuple-element.61, f32[512,24]{0,1:T(8,128)} %get-tuple-element.71, f32[512,24]{0,1:T(8,128)} %get-tuple-element.70, f32[512,24]{0,1:T(8,128)} %get-tuple-element.69, f32[512,24]{0,1:T(8,128)} %get-tuple-element.68, ...), kind=kOutput, calls=%fused_computation.37 | convolution fusion | flops 2433220608 | bytes 26263552 | tf_op jit(solution)/shard_map/qhk,khd->qhd/dot_general | solution.py:35
  177.4 6.6 %copy.101 = f32[512,24,128]{2,1,0:T(8,128)} copy(f32[512,24,128]{0,2,1:T(8,128)} %fusion.36) | data formatting | bytes 12582912 | tf_op jit(solution)/shard_map/add | solution.py:45
  184.0 6.0 %all-to-all-start = ((f32[8,64,24,128]{3,2,1,0:T(8,128)}), f32[8,64,24,128]{3,2,1,0:T(8,128)}, u32[]{:S(2)}, u32[]{:S(2)}) async-start(f32[8,64,24,128]{3,2,1,0:T(8,128)} %bitcast.107), calls=%async_computation | async-start | bytes 12582912 | tf_op jit(solution)/shard_map/all_to_all | solution.py:131
  190.0 0.5 broadcast.113
  190.5 1.6 reduce.2
  192.2 0.8 reduce.3
  193.3 132.3 %all-to-all-done = f32[8,64,24,128]{3,2,1,0:T(8,128)} async-done(((f32[8,64,24,128]{3,2,1,0:T(8,128)}), f32[8,64,24,128]{3,2,1,0:T(8,128)}, u32[]{:S(2)}, u32[]{:S(2)}) %all-to-all-start) | async-done | bytes 6291488 | tf_op jit(solution)/shard_map/all_to_all | solution.py:131
  325.6 4.5 %multiply_reduce_fusion = f32[64,24,128]{2,1,0:T(8,128)S(1)} fusion(f32[8,64,24,128]{3,2,1,0:T(8,128)} %all-to-all-done, f32[8,64,24]{2,1,0:T(8,128)S(1)} %copy.103), kind=kLoop, calls=%fused_computation.39 | loop fusion | flops 2949120 | bytes 7127040 | tf_op jit(solution)/shard_map/reduce_sum | solution.py:152
  330.4 0.8 copy.126
  331.9 1.1 convolution_reduce_fusion
  333.1 57.4 %all-gather.4.cloned.1.call-done = bf16[512,3072]{1,0:T(8,128)(2,1)} async-done(((bf16[64,3072]{1,0:T(8,128)(2,1)}), bf16[512,3072]{1,0:T(8,128)(2,1)}) %all-gather.4.cloned.1.call-update) | async-done | bytes 3145744 | tf_op jit(solution)/shard_map/all_gather | solution.py:155
  390.4 6.8 %fusion.45 = bf16[1,512,768]{2,1,0:T(8,128)(2,1)} fusion(bf16[512,3072]{1,0:T(8,128)(2,1)} %all-gather.4.cloned.1.call-done, bf16[3072,768]{1,0:T(8,128)(2,1)} %param.18, f32[768]{0:T(1024)S(1)} %convolution_reduce_fusion), kind=kOutput, calls=%fused_computation.50 | convolution fusion | flops 2416705536 | bytes 8653824 | tf_op jit(solution)/shard_map/dot_general | solution.py:154
  (31 shorter events, 1.2 us)
Async XLA Ops:
  6.5 325.4 %copy-start = (f32[1000,768]{1,0:T(8,128)S(1)}, f32[1000,768]{1,0:T(8,128)}, u32[]{:S(2)}) copy-start(f32[1000,768]{1,0:T(8,128)} %param.19) | copy-start | bytes 9216004
  6.5 65.8 %all-gather.6.cloned.1.call-start = ((), (), s32[]{:S(2)}) async-start(), calls=%async_computation.4 | async-start | bytes 3538944 | tf_op jit(solution)/shard_map/all_gather | solution.py:116
  7.3 9.5 %collective-permute-start = (bf16[2,64,3072]{2,1,0:T(8,128)(2,1)}, bf16[2,64,3072]{2,1,0:T(8,128)(2,1)}, u32[]{:S(2)}, u32[]{:S(2)}) collective-permute-start(bf16[2,64,3072]{2,1,0:T(8,128)(2,1)} %bitcast.118), channel_id=1, source_target_pairs={{0,8},{1,9},{2,10},{3,11},{4,12},{5,13},{6,14},{7,15},{16,24},{17,... | collective-permute-start | bytes 2359304 | tf_op jit(solution)/shard_map/ppermute | solution.py:19
  80.4 2.7 copy-start.1
  80.4 2.7 copy-start.3
  111.7 39.0 %copy-start.2 = (bf16[1,1,64,3072]{3,2,1,0:T(8,128)(2,1)S(1)}, bf16[1,1,64,3072]{3,2,1,0:T(8,128)(2,1)}, u32[]{:S(2)}) copy-start(bf16[1,1,64,3072]{3,2,1,0:T(8,128)(2,1)} %get-tuple-element.83) | copy-start | bytes 1179652
  146.7 10.8 %all-to-all-start.1 = ((f32[8,1,1536]{2,1,0:T(1,128)}), f32[8,1,1536]{2,1,0:T(1,128)}, u32[]{:S(2)}, u32[]{:S(2)}) async-start(f32[8,1,1536]{2,1,0:T(1,128)} %reshape.80), calls=%async_computation.1 | async-start | bytes 98304 | tf_op jit(solution)/shard_map/all_to_all | solution.py:138
  157.5 26.5 %all-to-all-start.2 = ((f32[8,1,1536]{2,1,0:T(1,128)}), f32[8,1,1536]{2,1,0:T(1,128)S(1)}, u32[]{:S(2)}, u32[]{:S(2)}) async-start(f32[8,1,1536]{2,1,0:T(1,128)} %reshape.82), calls=%async_computation.2 | async-start | bytes 98304 | tf_op jit(solution)/shard_map/all_to_all | solution.py:141
  184.0 141.6 %all-to-all-start = ((f32[8,64,24,128]{3,2,1,0:T(8,128)}), f32[8,64,24,128]{3,2,1,0:T(8,128)}, u32[]{:S(2)}, u32[]{:S(2)}) async-start(f32[8,64,24,128]{3,2,1,0:T(8,128)} %bitcast.107), calls=%async_computation | async-start | bytes 12582912 | tf_op jit(solution)/shard_map/all_to_all | solution.py:131
  190.0 200.5 %all-gather.4.cloned.1.call-start = ((), (), s32[]{:S(2)}) async-start(), calls=%async_computation.3 | async-start | bytes 3538944 | tf_op jit(solution)/shard_map/all_gather | solution.py:155
Sparse Core Ops, SparseCore 0:
  9.5 62.7 all-gather.5
  331.4 59.0 all-gather.3
where the time goes:
time: 406 us; the launch traced here: 404 us
  waiting for transfers between devices  245 us (60%)
  matrix products  53.7 us (13%)
  local copies, waits for them, and re-layouts  53.3 us (13%)
  other arithmetic  18.4 us (5%)
  starting transfers between devices  17.5 us (4%)
  between operations  16.2 us (4%)
    all_to_all x1, waiting for transfers between devices, on_device(): lax.all_to_all(output.reshape(tp_count, local_rows, H, HD), 'tp', split_a...  132 us
    all_gather x1, waiting for transfers between devices, on_device(): lax.all_gather(attended, 'tp', axis=0, tiled=True)  57.4 us
    all_gather x1, waiting for transfers between devices, on_device(): piece = lax.all_gather(query[0], 'tp', axis=0, tiled=True)  52.7 us
    dot_general x3, matrix products, head_block(): jnp.einsum('qhk,khd->qhd', weights, value_heads, precision=lax.Precision....  32.9 us
    cond x2, local copies, waits for them, and re-layouts, attend_all(): lax.cond(jnp.any(live_rows), lambda: head_block(queries, key_rows, value_...  13.1 us
    dot_general x3, matrix products, head_block(): jnp.einsum('qhd,khd->qhk', queries, key_heads, preferred_element_type=jnp...  11.8 us
    another operation x2, local copies, waits for them, and re-layouts  9.51 us
    reduce_sum x3, other arithmetic, head_block(): weight_sum = jnp.sum(weights, axis=2)  8.84 us
  transfers between devices with their start and end apart: 6, of which 4 were waited for; matrix products, arithmetic and copies ran while one was open for 10% of the time, Pallas kernels for 0%

commit v1 on v0

--- a/solution.py
+++ b/solution.py
@@ -1,8 +1,11 @@
+import functools
 import math
 
 import jax
 import jax.numpy as jnp
 from jax import lax
+from jax.experimental import pallas as pl
+from jax.experimental.pallas import tpu as pltpu
 from jax.sharding import PartitionSpec as P
 
 H = 24
@@ -163,9 +166,347 @@
     return (projected * gate_row).astype(jnp.bfloat16)[None]
 
 
+MESH = pl.DeviceIdType.MESH
+
+
+def fused_kernel(
+    n,
+    heads,
+    mask_ref,
+    blocks_ref,
+    query_in,
+    fresh_in,
+    history_in,
+    weight_in,
+    gate_ref,
+    out_ref,
+    kv,
+    queries,
+    gathered,
+    weight,
+    bias,
+    total,
+    in_send,
+    in_recv,
+    pass_send,
+    pass_recv,
+    gather_send,
+    gather_recv,
+    local_sem,
+):
+    me = lax.axis_index("tp")
+    core = lax.axis_index("stretch")
+    partner = {"stretch": 1 - core}
+    line = n // 2
+    spot, side = me // 2, me % 2
+    local_rows = query_in.shape[1]
+    history_rows = history_in.shape[1]
+    row_count = n * local_rows
+    history_total = n * history_rows
+    other_base = history_total
+    own_base = history_total + row_count
+    block_count = mask_ref.shape[1]
+
+    barrier = pltpu.get_barrier_semaphore()
+    for offset in range(1, n):
+        pl.semaphore_signal(
+            barrier, inc=1, device_id={"tp": lax.rem(me + offset, n)}, device_id_type=MESH
+        )
+    pl.semaphore_signal(barrier, inc=1, device_id=partner, device_id_type=MESH)
+    pl.semaphore_wait(barrier, n)
+
+    def remote(source, target, send, recv, device):
+        return pltpu.make_async_remote_copy(
+            src_ref=source,
+            dst_ref=target,
+            send_sem=send,
+            recv_sem=recv,
+            device_id=device,
+            device_id_type=MESH,
+        )
+
+    def columns(owner, head):
+        return pl.ds(pl.multiple_of((owner * heads + head) * HD, HD), HD)
+
+    def history_span(source):
+        return pl.ds(pl.multiple_of(source * history_rows, history_rows), history_rows)
+
+    def fresh_span(base, source):
+        return pl.ds(pl.multiple_of(base + source * local_rows, local_rows), local_rows)
+
+    def inbound(head, source, target):
+        wide = columns(target, head)
+        device = {"tp": target}
+        return (
+            remote(
+                history_in.at[core, :, wide],
+                kv.at[head, core, history_span(source), :],
+                in_send.at[0, head, target],
+                in_recv.at[0, head, source],
+                device,
+            ),
+            remote(
+                fresh_in.at[:, 0, :, wide],
+                kv.at[head, :, fresh_span(own_base, source), :],
+                in_send.at[1, head, target],
+                in_recv.at[1, head, source],
+                device,
+            ),
+            remote(
+                query_in.at[0, :, wide],
+                queries.at[head, fresh_span(0, source), :],
+                in_send.at[2, head, target],
+                in_recv.at[2, head, source],
+                device,
+            ),
+        )
+
+    def passed_history(head, source, which):
+        place = kv.at[head, which, history_span(source), :]
+        return remote(
+            place, place, pass_send.at[0, head, source], pass_recv.at[0, head, source], partner
+        )
+
+    def passed_fresh(head, source):
+        return remote(
+            kv.at[head, :, fresh_span(own_base, source), :],
+            kv.at[head, :, fresh_span(other_base, source), :],
+            pass_send.at[1, head, source],
+            pass_recv.at[1, head, source],
+            partner,
+        )
+
+    def own_fresh(head):
+        return remote(
+            fresh_in.at[:, 0, :, columns(me, head)],
+            kv.at[head, :, fresh_span(other_base, me), :],
+            pass_send.at[1, head, me],
+            pass_recv.at[1, head, me],
+            partner,
+        )
+
+    def local_copies(head):
+        wide = columns(me, head)
+        pairs = (
+            (history_in.at[:, :, wide], kv.at[head, :, history_span(me), :]),
+            (fresh_in.at[:, 0, :, wide], kv.at[head, :, fresh_span(own_base, me), :]),
+            (query_in.at[0, :, wide], queries.at[head, fresh_span(0, me), :]),
+            (weight_in.at[:, head], weight.at[head]),
+        )
+        return [
+            pltpu.make_async_copy(source, target, local_sem.at[place, head])
+            for place, (source, target) in enumerate(pairs)
+        ]
+
+    for head in range(heads):
+        for offset in range(1, n):
+            for copy in inbound(head, me, lax.rem(me + offset, n)):
+                copy.start()
+        own_fresh(head).start()
+        for copy in local_copies(head):
+            copy.start()
+
+    live = blocks_ref[0] * BLK
+    positions = lax.broadcasted_iota(jnp.int32, (1, history_total), 1)
+    history_bias = jnp.where(positions < live, 0.0, NEGATIVE)
+    for block in range(block_count):
+        bias[block : block + 1, 0:history_total] = history_bias
+        for column in range(2 * block_count):
+            shown = jnp.full((1, BLK), mask_ref[0, block, column], jnp.int32)
+            begin = history_total + column * BLK
+            bias[block : block + 1, begin : begin + BLK] = jnp.where(shown > 0, 0.0, NEGATIVE)
+
+    unit = math.log2(math.e) / math.sqrt(HD)
+
+    def attend(head):
+        def step(block, carry):
+            rows = pl.ds(pl.multiple_of(block * BLK, BLK), BLK)
+            scores = lax.dot_general(
+                queries[head, rows, :],
+                kv[head, 0],
+                (((1,), (1,)), ((), ())),
+                preferred_element_type=jnp.float32,
+            )
+            scores = scores * unit + bias[pl.ds(block, 1), :]
+            peak = jnp.max(scores, axis=1, keepdims=True)
+            weights = jnp.exp2(scores - peak)
+            weight_sum = jnp.sum(weights, axis=1, keepdims=True)
+            output = jnp.dot(
+                weights.astype(jnp.bfloat16), kv[head, 1], preferred_element_type=jnp.float32
+            )
+            gathered[head, me, rows, :] = (output / weight_sum).astype(jnp.bfloat16)
+            return carry
+
+        lax.fori_loop(0, block_count, step, 0)
+
+    def hop(head, block, way):
+        place = gathered.at[head, block]
+        target = (me + 2, me - 2, me + 1 - 2 * side)[way]
+        return remote(
+            place,
+            place,
+            gather_send.at[way, head, block],
+            gather_recv.at[head, block],
+            {"tp": target},
+        )
+
+    def launch(head, block, up, down):
+        if up:
+            pl.when(spot < line - 1)(lambda: hop(head, block, 0).start())
+        if down:
+            pl.when(spot > 0)(lambda: hop(head, block, 1).start())
+        hop(head, block, 2).start()
+
+    def relay(head):
+        for far in range(1, line):
+
+            @pl.when(spot >= far)
+            def _():
+                block = me - 2 * far
+                hop(head, block, 2).wait_recv()
+                launch(head, block, True, False)
+
+            @pl.when(spot + far < line)
+            def _():
+                block = me + 2 * far
+                hop(head, block, 2).wait_recv()
+                launch(head, block, False, True)
+
+    def finish(head):
+        for place in range(line):
+            hop(head, 2 * place + 1 - side, 2).wait_recv()
+
+    def project(head):
+        last = head == heads - 1
+
+        def step(block, carry):
+            rows = pl.ds(pl.multiple_of(block * BLK, BLK), BLK)
+            left = jnp.concatenate([gathered[head, source, rows, :] for source in range(n)], axis=1)
+            right = weight[head].reshape(n * HD, weight.shape[3])
+            part = jnp.dot(left, right, preferred_element_type=jnp.float32)
+            if head > 0:
+                part = part + total[rows, :]
+            if last:
+                out_ref[0, rows, :] = (part * gate_ref[...]).astype(out_ref.dtype)
+            else:
+                total[rows, :] = part
+            return carry
+
+        lax.fori_loop(0, block_count, step, 0)
+
+    for head in range(heads):
+        mine = local_copies(head)
+        for copy in mine[:3]:
+            copy.wait()
+        for offset in range(1, n):
+            source = lax.rem(me + n - offset, n)
+            arrivals = inbound(head, source, me)
+            arrivals[0].wait_recv()
+            passed_history(head, source, core).start()
+            arrivals[1].wait_recv()
+            passed_fresh(head, source).start()
+            arrivals[2].wait_recv()
+        for offset in range(1, n):
+            source = lax.rem(me + n - offset, n)
+            passed_history(head, source, 1 - core).wait_recv()
+            passed_fresh(head, source).wait_recv()
+        own_fresh(head).wait_recv()
+        attend(head)
+        launch(head, me, True, True)
+        if head > 0:
+            relay(head - 1)
+            finish(head - 1)
+            local_copies(head - 1)[3].wait()
+            project(head - 1)
+    relay(heads - 1)
+    finish(heads - 1)
+    local_copies(heads - 1)[3].wait()
+    project(heads - 1)
+
+    for head in range(heads):
+        for offset in range(1, n):
+            source = lax.rem(me + n - offset, n)
+            for copy in inbound(head, me, lax.rem(me + offset, n)):
+                copy.wait_send()
+            passed_history(head, source, core).wait_send()
+            passed_fresh(head, source).wait_send()
+        own_fresh(head).wait_send()
+        for way, allowed in ((0, spot < line - 1), (1, spot > 0)):
+
+            @pl.when(allowed)
+            def _():
+                hop(head, me, way).wait_send()
+
+        hop(head, me, 2).wait_send()
+        for far in range(1, line):
+
+            @pl.when(spot >= far)
+            def _():
+                block = me - 2 * far
+                pl.when(spot < line - 1)(lambda: hop(head, block, 0).wait_send())
+                hop(head, block, 2).wait_send()
+
+            @pl.when(spot + far < line)
+            def _():
+                block = me + 2 * far
+                pl.when(spot > 0)(lambda: hop(head, block, 1).wait_send())
+                hop(head, block, 2).wait_send()
+
+
+def on_device_fused(
+    query, stretch_kv, history_kv, block_mask, noise_level, history_blocks, out_weight, gate_table
+):
+    n = lax.axis_size("tp")
+    heads = H // n
+    local_rows, history_rows = query.shape[1], history_kv.shape[1]
+    row_count = n * local_rows
+    key_count = n * history_rows + 2 * row_count
+    wide = out_weight.shape[1]
+    block_count = block_mask.shape[1]
+    gate_row = lax.dynamic_slice(gate_table, (noise_level[0], 0), (1, wide))
+    anywhere = pl.BlockSpec(memory_space=pl.ANY)
+    scalars = pl.BlockSpec(memory_space=pltpu.SMEM)
+    vector = pl.BlockSpec(memory_space=pltpu.VMEM)
+    dma = pltpu.SemaphoreType.DMA
+    return pl.pallas_call(
+        functools.partial(fused_kernel, n, heads),
+        out_shape=jax.ShapeDtypeStruct((1, row_count, wide), jnp.bfloat16),
+        in_specs=[scalars, scalars, anywhere, anywhere, anywhere, anywhere, vector],
+        out_specs=vector,
+        scratch_shapes=[
+            pltpu.VMEM((heads, 2, key_count, HD), jnp.bfloat16),
+            pltpu.VMEM((heads, row_count, HD), jnp.bfloat16),
+            pltpu.VMEM((heads, n, row_count, HD), jnp.bfloat16),
+            pltpu.VMEM((heads, n, HD, wide), jnp.bfloat16),
+            pltpu.VMEM((block_count, key_count), jnp.float32),
+            pltpu.VMEM((row_count, wide), jnp.float32),
+            dma((3, heads, n)),
+            dma((3, heads, n)),
+            dma((2, heads, n)),
+            dma((2, heads, n)),
+            dma((3, heads, n)),
+            dma((heads, n)),
+            dma((4, heads)),
+        ],
+        compiler_params=pltpu.CompilerParams(
+            collective_id=0, has_side_effects=True, vmem_limit_bytes=60 * 1024 * 1024
+        ),
+    )(
+        block_mask,
+        history_blocks,
+        query,
+        stretch_kv,
+        history_kv,
+        out_weight.reshape(n, heads, HD, wide),
+        gate_row,
+    )
+
+
 def solution(mesh):
+    count = mesh.shape["tp"]
+    fits = H % count == 0 and count % 2 == 0 and mesh.shape["stretch"] == 2
     return jax.shard_map(
-        on_device,
+        on_device_fused if fits else on_device,
         mesh=mesh,
         in_specs=(
             P(("rep", "stretch"), "tp", None),

time: 406 us -> 125 us (0.31)
  waiting for transfers between devices: 245 us -> 0 us
  Pallas kernels: 0 us -> 120 us
  matrix products: 53.7 us -> 0 us
  local copies, waits for them, and re-layouts: 53.3 us -> 2.94 us
  other arithmetic: 18.4 us -> 0 us
  starting transfers between devices: 17.5 us -> 0 us
  between operations: 16.2 us -> 1.6 us
    all_to_all x3 -> x0, waiting for transfers between devices: 134 us -> none  [the longest x1 132 us: on_device(): lax.all_to_all(output.reshape(tp_count, local_rows, H, HD), 'tp', split_a...]
    pallas_call x0 -> x1, Pallas kernels: none -> 120 us  [on_device_fused(): pl.pallas_call(functools.partial(fused_kernel, n, heads), out_shape=jax.S...]
    all_gather x2 -> x0, waiting for transfers between devices: 110 us -> none  [the longest x1 57.4 us: on_device(): lax.all_gather(attended, 'tp', axis=0, tiled=True)]
    dot_general x9 -> x0, matrix products: 53.7 us -> none  [the longest x3 32.9 us: head_block(): jnp.einsum('qhk,khd->qhd', weights, value_heads, precision=lax.Precision....]
    all_to_all x3 -> x0, starting transfers between devices: 14.1 us -> none  [the longest x1 6 us: on_device(): lax.all_to_all(output.reshape(tp_count, local_rows, H, HD), 'tp', split_a...]
    reduce_sum x5 -> x0, other arithmetic: 13.4 us -> none  [the longest x3 8.84 us: head_block(): weight_sum = jnp.sum(weights, axis=2)]
    cond x2 -> x0, local copies, waits for them, and re-layouts: 13.1 us -> none  [attend_all(): lax.cond(jnp.any(live_rows), lambda: head_block(queries, key_rows, value_...]
    slice x6 -> x0, local copies, waits for them, and re-layouts: 10.1 us -> none  [the longest x4 7.2 us: on_device(): fresh_values = jnp.concatenate([older_pair[1], own_pair[1]], 0)]
  transfers between devices with their start and end apart: 6 -> 0, of which waited for: 4 -> 0; matrix products, arithmetic and copies ran while one was open for 10% -> 0% of each run, Pallas kernels for 0% -> 0%
where the time goes in v1:
time: 125 us; the launch traced here: 124 us
  Pallas kernels  120 us (96%)
  local copies, waits for them, and re-layouts  2.94 us (2%)
  between operations  1.6 us (1%)
    pallas_call x1, Pallas kernels, on_device_fused(): pl.pallas_call(functools.partial(fused_kernel, n, heads), out_shape=jax.S...  120 us

profile of v1, /device:TPU:0, one launch (start us, length us, event | category | flops | bytes accessed | tf_op | source)
XLA Modules:
  0.0 124.3 jit_solution(1208607574461408387)
XLA Ops:
  0.0 0.0 copy-start
  1.6 0.3 copy-done
  1.9 0.6 constant_dynamic-slice_fusion.gate_ref
  2.5 119.8 %shard_map.82 = bf16[1,512,768]{2,1,0:T(8,128)(2,1)} custom-call(s32[1,4,8]{2,1,0:T(4,128)} %mask_ref.1, s32[1]{0:T(128)S(6)} %copy.11.blocks_ref, bf16[1,64,3072]{2,1,0:T(8,128)(2,1)} %query_in.1, bf16[2,1,64,3072]{3,2,1,0:T(8,128)(2,1)} %fresh_in.1, bf16[2,256,3072]{2,1,0:T(8,128)(2,1)} %history_in.1, bf16[8,3,128,768]{3,2,1,0:T(8,128)(2,1)} %bitcast.5, ...), custom_call_target="tpu_custom_call" | custom-call | tf_op jit(solution)/shard_map/pallas_call | solution.py:471
  122.2 2.1 %copy.12 = bf16[1,512,768]{2,1,0:T(8,128)(2,1)} copy(bf16[1,512,768]{2,1,0:T(8,128)(2,1)} %shard_map.82) | data formatting | bytes 1572864
Async XLA Ops:
  0.0 1.9 %copy-start = (f32[1000,768]{1,0:T(8,128)S(1)}, f32[1000,768]{1,0:T(8,128)}, u32[]{:S(2)}) copy-start(f32[1000,768]{1,0:T(8,128)} %param.15) | copy-start | bytes 9216004

commit v2 on v1

--- a/solution.py
+++ b/solution.py
@@ -167,6 +167,26 @@
 
 
 MESH = pl.DeviceIdType.MESH
+WINDOW = 3
+PIECES = 2
+LAG = 0
+
+
+def exchange_order(n):
+    far, near = list(range(n // 2, n)), list(range(1, n // 2))
+    order = []
+    for place, code in enumerate(far):
+        order += [code] + near[place : place + 1]
+    return order
+
+
+def crossed(me, code, n):
+    partner, bit = 0, 1
+    while bit < n:
+        digit = lax.rem(me // bit, 2)
+        partner = partner + bit * (1 - digit if code & bit else digit)
+        bit *= 2
+    return partner
 
 
 def fused_kernel(
@@ -206,6 +226,8 @@
     other_base = history_total
     own_base = history_total + row_count
     block_count = mask_ref.shape[1]
+    piece_blocks = block_count // PIECES
+    piece_rows = piece_blocks * BLK
 
     barrier = pltpu.get_barrier_semaphore()
     for offset in range(1, n):
@@ -285,26 +307,31 @@
             partner,
         )
 
-    def local_copies(head):
+    def local_copy(head, place):
         wide = columns(me, head)
-        pairs = (
+        source, target = (
             (history_in.at[:, :, wide], kv.at[head, :, history_span(me), :]),
             (fresh_in.at[:, 0, :, wide], kv.at[head, :, fresh_span(own_base, me), :]),
             (query_in.at[0, :, wide], queries.at[head, fresh_span(0, me), :]),
             (weight_in.at[:, head], weight.at[head]),
-        )
-        return [
-            pltpu.make_async_copy(source, target, local_sem.at[place, head])
-            for place, (source, target) in enumerate(pairs)
-        ]
-
+        )[place]
+        return pltpu.make_async_copy(source, target, local_sem.at[place, head])
+
+    peers = [crossed(me, code, n) for code in exchange_order(n)]
+    steps = [(head, peer) for head in range(heads) for peer in peers]
+
+    def send_step(index):
+        if index < len(steps):
+            head, peer = steps[index]
+            for copy in inbound(head, me, peer):
+                copy.start()
+
+    for index in range(WINDOW):
+        send_step(index)
     for head in range(heads):
-        for offset in range(1, n):
-            for copy in inbound(head, me, lax.rem(me + offset, n)):
-                copy.start()
         own_fresh(head).start()
-        for copy in local_copies(head):
-            copy.start()
+        for place in range(4):
+            local_copy(head, place).start()
 
     live = blocks_ref[0] * BLK
     positions = lax.broadcasted_iota(jnp.int32, (1, history_total), 1)
@@ -318,7 +345,7 @@
 
     unit = math.log2(math.e) / math.sqrt(HD)
 
-    def attend(head):
+    def attend(head, piece):
         def step(block, carry):
             rows = pl.ds(pl.multiple_of(block * BLK, BLK), BLK)
             scores = lax.dot_general(
@@ -337,46 +364,44 @@
             gathered[head, me, rows, :] = (output / weight_sum).astype(jnp.bfloat16)
             return carry
 
-        lax.fori_loop(0, block_count, step, 0)
-
-    def hop(head, block, way):
-        place = gathered.at[head, block]
+        lax.fori_loop(piece * piece_blocks, (piece + 1) * piece_blocks, step, 0)
+
+    def hop(head, block, way, piece):
+        place = gathered.at[head, block, piece * piece_rows : (piece + 1) * piece_rows, :]
         target = (me + 2, me - 2, me + 1 - 2 * side)[way]
         return remote(
             place,
             place,
-            gather_send.at[way, head, block],
-            gather_recv.at[head, block],
+            gather_send.at[way, head, block * PIECES + piece],
+            gather_recv.at[head, block * PIECES + piece],
             {"tp": target},
         )
 
-    def launch(head, block, up, down):
+    def launch(head, block, up, down, piece):
         if up:
-            pl.when(spot < line - 1)(lambda: hop(head, block, 0).start())
+            pl.when(spot < line - 1)(lambda: hop(head, block, 0, piece).start())
         if down:
-            pl.when(spot > 0)(lambda: hop(head, block, 1).start())
-        hop(head, block, 2).start()
-
-    def relay(head):
-        for far in range(1, line):
-
-            @pl.when(spot >= far)
-            def _():
-                block = me - 2 * far
-                hop(head, block, 2).wait_recv()
-                launch(head, block, True, False)
-
-            @pl.when(spot + far < line)
-            def _():
-                block = me + 2 * far
-                hop(head, block, 2).wait_recv()
-                launch(head, block, False, True)
-
-    def finish(head):
+            pl.when(spot > 0)(lambda: hop(head, block, 1, piece).start())
+        hop(head, block, 2, piece).start()
+
+    def relay(head, far, piece):
+        @pl.when(spot >= far)
+        def _():
+            block = me - 2 * far
+            hop(head, block, 2, piece).wait_recv()
+            launch(head, block, True, False, piece)
+
+        @pl.when(spot + far < line)
+        def _():
+            block = me + 2 * far
+            hop(head, block, 2, piece).wait_recv()
+            launch(head, block, False, True, piece)
+
+    def finish(head, piece):
         for place in range(line):
-            hop(head, 2 * place + 1 - side, 2).wait_recv()
-
-    def project(head):
+            hop(head, 2 * place + 1 - side, 2, piece).wait_recv()
+
+    def project(head, piece):
         last = head == heads - 1
 
         def step(block, carry):
@@ -392,65 +417,77 @@
                 total[rows, :] = part
             return carry
 
-        lax.fori_loop(0, block_count, step, 0)
-
+        lax.fori_loop(piece * piece_blocks, (piece + 1) * piece_blocks, step, 0)
+
+    relay_after = {len(peers) - 1 - 2 * (line - 1 - LAG - far): far for far in range(1, line - LAG)}
     for head in range(heads):
-        mine = local_copies(head)
-        for copy in mine[:3]:
-            copy.wait()
-        for offset in range(1, n):
-            source = lax.rem(me + n - offset, n)
+        for place in range(3):
+            local_copy(head, place).wait()
+        for place, source in enumerate(peers):
             arrivals = inbound(head, source, me)
             arrivals[0].wait_recv()
             passed_history(head, source, core).start()
             arrivals[1].wait_recv()
             passed_fresh(head, source).start()
             arrivals[2].wait_recv()
-        for offset in range(1, n):
-            source = lax.rem(me + n - offset, n)
+            send_step(head * len(peers) + place + WINDOW)
+            if head > 0 and place in relay_after:
+                for piece in range(PIECES):
+                    relay(head - 1, relay_after[place], piece)
+        for source in peers:
             passed_history(head, source, 1 - core).wait_recv()
             passed_fresh(head, source).wait_recv()
         own_fresh(head).wait_recv()
-        attend(head)
-        launch(head, me, True, True)
+        for piece in range(PIECES):
+            attend(head, piece)
+            launch(head, me, True, True, piece)
         if head > 0:
-            relay(head - 1)
-            finish(head - 1)
-            local_copies(head - 1)[3].wait()
-            project(head - 1)
-    relay(heads - 1)
-    finish(heads - 1)
-    local_copies(heads - 1)[3].wait()
-    project(heads - 1)
+            if LAG:
+                for piece in range(PIECES):
+                    relay(head - 1, line - 1, piece)
+            local_copy(head - 1, 3).wait()
+            for piece in range(PIECES):
+                finish(head - 1, piece)
+                project(head - 1, piece)
+    for far in range(1, line):
+        for piece in range(PIECES):
+            relay(heads - 1, far, piece)
+    local_copy(heads - 1, 3).wait()
+    for piece in range(PIECES):
+        finish(heads - 1, piece)
+        project(heads - 1, piece)
 
     for head in range(heads):
-        for offset in range(1, n):
-            source = lax.rem(me + n - offset, n)
-            for copy in inbound(head, me, lax.rem(me + offset, n)):
+        for source in peers:
+            for copy in inbound(head, me, source):
                 copy.wait_send()
             passed_history(head, source, core).wait_send()
             passed_fresh(head, source).wait_send()
         own_fresh(head).wait_send()
-        for way, allowed in ((0, spot < line - 1), (1, spot > 0)):
-
-            @pl.when(allowed)
+        for piece in range(PIECES):
+
+            @pl.when(spot < line - 1)
             def _():
-                hop(head, me, way).wait_send()
-
-        hop(head, me, 2).wait_send()
-        for far in range(1, line):
-
-            @pl.when(spot >= far)
+                hop(head, me, 0, piece).wait_send()
+
+            @pl.when(spot > 0)
             def _():
-                block = me - 2 * far
-                pl.when(spot < line - 1)(lambda: hop(head, block, 0).wait_send())
-                hop(head, block, 2).wait_send()
-
-            @pl.when(spot + far < line)
-            def _():
-                block = me + 2 * far
-                pl.when(spot > 0)(lambda: hop(head, block, 1).wait_send())
-                hop(head, block, 2).wait_send()
+                hop(head, me, 1, piece).wait_send()
+
+            hop(head, me, 2, piece).wait_send()
+            for far in range(1, line):
+
+                @pl.when(spot >= far)
+                def _():
+                    block = me - 2 * far
+                    pl.when(spot < line - 1)(lambda: hop(head, block, 0, piece).wait_send())
+                    hop(head, block, 2, piece).wait_send()
+
+                @pl.when(spot + far < line)
+                def _():
+                    block = me + 2 * far
+                    pl.when(spot > 0)(lambda: hop(head, block, 1, piece).wait_send())
+                    hop(head, block, 2, piece).wait_send()
 
 
 def on_device_fused(
@@ -484,8 +521,8 @@
             dma((3, heads, n)),
             dma((2, heads, n)),
             dma((2, heads, n)),
-            dma((3, heads, n)),
-            dma((heads, n)),
+            dma((3, heads, n * PIECES)),
+            dma((heads, n * PIECES)),
             dma((4, heads)),
         ],
         compiler_params=pltpu.CompilerParams(
@@ -504,7 +541,7 @@
 
 def solution(mesh):
     count = mesh.shape["tp"]
-    fits = H % count == 0 and count % 2 == 0 and mesh.shape["stretch"] == 2
+    fits = H % count == 0 and count & (count - 1) == 0 and count > 2 and mesh.shape["stretch"] == 2
     return jax.shard_map(
         on_device_fused if fits else on_device,
         mesh=mesh,

time: 125 us -> 110 us (0.88)
  Pallas kernels: 120 us -> 105 us
    pallas_call x1, Pallas kernels: 120 us -> 105 us  [on_device_fused(): pl.pallas_call(functools.partial(fused_kernel, n, heads), out_shape=jax.S...]
where the time goes in v2:
time: 110 us; the launch traced here: 109 us
  Pallas kernels  105 us (95%)
  local copies, waits for them, and re-layouts  2.94 us (3%)
  between operations  1.6 us (1%)
    pallas_call x1, Pallas kernels, on_device_fused(): pl.pallas_call(functools.partial(fused_kernel, n, heads), out_shape=jax.S...  105 us
    unnamed x3, local copies, waits for them, and re-layouts  2.35 us

profile of v2, /device:TPU:0, one launch (start us, length us, event | category | flops | bytes accessed | tf_op | source)
XLA Modules:
  0.0 109.4 jit_solution(9377707847665021395)
XLA Ops:
  0.0 0.0 copy-start
  1.6 0.3 copy-done
  1.9 0.6 constant_dynamic-slice_fusion.gate_ref
  2.5 104.9 %shard_map.82 = bf16[1,512,768]{2,1,0:T(8,128)(2,1)} custom-call(s32[1,4,8]{2,1,0:T(4,128)} %mask_ref.1, s32[1]{0:T(128)S(6)} %copy.11.blocks_ref, bf16[1,64,3072]{2,1,0:T(8,128)(2,1)} %query_in.1, bf16[2,1,64,3072]{3,2,1,0:T(8,128)(2,1)} %fresh_in.1, bf16[2,256,3072]{2,1,0:T(8,128)(2,1)} %history_in.1, bf16[8,3,128,768]{3,2,1,0:T(8,128)(2,1)} %bitcast.5, ...), custom_call_target="tpu_custom_call" | custom-call | tf_op jit(solution)/shard_map/pallas_call | solution.py:508
  107.4 2.1 %copy.12 = bf16[1,512,768]{2,1,0:T(8,128)(2,1)} copy(bf16[1,512,768]{2,1,0:T(8,128)(2,1)} %shard_map.82) | data formatting | bytes 1572864
Async XLA Ops:
  0.0 1.9 %copy-start = (f32[1000,768]{1,0:T(8,128)S(1)}, f32[1000,768]{1,0:T(8,128)}, u32[]{:S(2)}) copy-start(f32[1000,768]{1,0:T(8,128)} %param.15) | copy-start | bytes 9216004
